TPU v7x, 32 devices: a whole 2x2x4 slice. The times are simulated.
32 devices in a mesh: row: 4 (over z), col: 8 (over y, x, core).
Axes of the slice: x: 2, y: 2, z: 4, core: 2. Of those that a mesh axis runs over, the one named last changes fastest.
Arguments:
- points: float32 [16, 32768], P(None, ('row', 'col')), may hold values from -6 to 6
- inverse_scales: float32 [16], replicated, may hold values from 0.05 to 31.255105
- probe_signs: int32 [32768, 128], P(('row', 'col')), may hold values 0 or 1
Outputs:
- trace_terms: float32 [128], replicated
- logdet_terms: float32 [128], replicated
All inputs are finite; a program needn't handle non-finite values. No bound on the sum of `probe_signs` on one device may be relied on, other than what follows from the above.
Results may differ from a plain program's by a relative error of at most 0.0014.
Values may be sent and summed in bfloat16 or wider, within the bound.
A program may use at most 128 MiB of HBM per device.

v0:
```python
import math
import jax
import jax.numpy as jnp
from jax import lax
from jax.sharding import PartitionSpec as P

STEPS = 3
epsilon = 1e-06
noise_level = 1.0
jacobi_sweeps = 6


def kernel_block(left_points, right_points):
    cross_term = lax.dot_general(
        left_points,
        right_points,
        (((0,), (0,)), ((), ())),
        precision=lax.Precision.HIGHEST,
        preferred_element_type=jnp.float32,
    )
    left_norms = jnp.sum(left_points * left_points, axis=0)
    right_norms = jnp.sum(right_points * right_points, axis=0)
    distance = jnp.maximum(left_norms[:, None] + right_norms[None, :] - 2.0 * cross_term, 0.0)
    return jnp.exp(-0.5 * distance).astype(jnp.bfloat16)


def form_blocks(row_points, col_points):
    total_rows = row_points.shape[1]
    block_rows = math.gcd(total_rows, 512)
    blocked = row_points.reshape(
        row_points.shape[0], total_rows // block_rows, block_rows
    ).transpose(1, 0, 2)
    stacked = lax.map(lambda block_points: kernel_block(block_points, col_points), blocked)
    return stacked.reshape(total_rows, col_points.shape[1])


def log_weight(alpha_list, beta_list):
    degree = len(alpha_list)
    width_probes = alpha_list[0].shape[0]
    zeros_row = jnp.zeros((width_probes,), jnp.float32)
    ones_row = jnp.ones((width_probes,), jnp.float32)
    matrix = []
    vectors = []
    for first_idx in range(degree):
        entries = []
        basis_row = []
        for second_idx in range(degree):
            if first_idx == second_idx:
                entries.append(alpha_list[first_idx])
                basis_row.append(ones_row)
            elif abs(first_idx - second_idx) == 1:
                entries.append(beta_list[min(first_idx, second_idx)])
                basis_row.append(zeros_row)
            else:
                entries.append(zeros_row)
                basis_row.append(zeros_row)
        matrix.append(entries)
        vectors.append(basis_row)
    for sweep_index in range(jacobi_sweeps):
        for first_idx in range(degree):
            for second_idx in range(first_idx + 1, degree):
                coupling = matrix[first_idx][second_idx]
                rotate_by = 0.5 * jnp.arctan2(
                    2.0 * coupling, matrix[second_idx][second_idx] - matrix[first_idx][first_idx]
                )
                cosine = jnp.cos(rotate_by)
                sine_val = jnp.sin(rotate_by)
                for row_idx in range(degree):
                    left_val = matrix[row_idx][first_idx]
                    right_val = matrix[row_idx][second_idx]
                    matrix[row_idx][first_idx] = cosine * left_val - sine_val * right_val
                    matrix[row_idx][second_idx] = sine_val * left_val + cosine * right_val
                    left_vec = vectors[row_idx][first_idx]
                    right_vec = vectors[row_idx][second_idx]
                    vectors[row_idx][first_idx] = cosine * left_vec - sine_val * right_vec
                    vectors[row_idx][second_idx] = sine_val * left_vec + cosine * right_vec
                for col_idx in range(degree):
                    upper_val = matrix[first_idx][col_idx]
                    lower_val = matrix[second_idx][col_idx]
                    matrix[first_idx][col_idx] = cosine * upper_val - sine_val * lower_val
                    matrix[second_idx][col_idx] = sine_val * upper_val + cosine * lower_val
    total = zeros_row
    for index_k in range(degree):
        total = total + vectors[0][index_k] * vectors[0][index_k] * jnp.log(
            matrix[index_k][index_k]
        )
    return total


def per_device(points, inverse_scales, probe_signs):
    scaled = points * inverse_scales[:, None]
    row_points = lax.all_gather(scaled, "col", axis=1, tiled=True)
    col_points = lax.all_gather(scaled, "row", axis=1, tiled=True)
    cached = form_blocks(row_points, col_points)
    direction = 2.0 * probe_signs.astype(jnp.float32) - 1.0
    basis_prev = jnp.zeros_like(direction)
    alpha_list = []
    beta_list = []
    for lanczos_step in range(STEPS):
        squares = lax.psum(jnp.sum(direction * direction, axis=0), ("row", "col"))
        vector_half = direction.astype(jnp.bfloat16)
        gathered = lax.all_gather(vector_half, "col", axis=0, tiled=True)
        image = (
            lax.psum_scatter(
                lax.dot_general(
                    cached, gathered, (((0,), (0,)), ((), ())), preferred_element_type=jnp.float32
                ).astype(jnp.bfloat16),
                "row",
                scatter_dimension=0,
                tiled=True,
            ).astype(jnp.float32)
            + noise_level * direction
        )
        curvature = lax.psum(jnp.sum(direction * image, axis=0), ("row", "col"))
        beta_now = jnp.sqrt(squares + epsilon)
        alpha_now = curvature / (beta_now * beta_now)
        alpha_list.append(alpha_now)
        beta_list.append(beta_now)
        if lanczos_step + 1 < STEPS:
            basis_now = direction / beta_now
            direction = image / beta_now - alpha_now * basis_now - beta_now * basis_prev
            basis_prev = basis_now
    logdet_terms = log_weight(alpha_list, beta_list[1:])
    return (alpha_list[0], logdet_terms)


def solution(mesh):
    in_specs = (P(None, ("row", "col")), P(), P(("row", "col"), None))
    out_specs = (P(), P())
    return jax.shard_map(
        per_device, mesh=mesh, in_specs=in_specs, out_specs=out_specs, check_vma=False
    )
```

profile of v0, /device:TPU:0, one launch (start us, length us, event | category | flops | bytes accessed | tf_op | source)
XLA Modules:
  0.0 559.0 jit_solution(14007900071963346204)
XLA Ops:
  7.2 0.0 all-gather.4.cloned.1.call-start
  7.2 1.8 fusion.8
  9.0 0.0 all-gather.4.cloned.1.call-update
  9.1 0.0 reduce-scatter.4.cloned.1.call-start
  9.1 0.9 broadcast_multiply_fusion
  10.0 15.6 %all_gather.16 = f32[16,4096]{1,0:T(8,128)S(1)} all-gather(f32[16,1024]{1,0:T(8,128)S(1)} %broadcast_multiply_fusion), channel_id=1, replica_groups=mesh['row'=4,'col'=8] {'row'}, dimensions={1}, use_global_device_ids=true | all-gather | bytes 327680 | tf_op jit(solution)/shard_map/all_gather | solution.py:93
  25.7 11.0 %all_gather.15 = f32[16,8192]{1,0:T(8,128)S(1)} all-gather(f32[16,1024]{1,0:T(8,128)S(1)} %broadcast_multiply_fusion), channel_id=1, replica_groups=mesh['row'=4,'col'=8] {'col'}, dimensions={1}, use_global_device_ids=true | all-gather | bytes 589824 | tf_op jit(solution)/shard_map/all_gather | solution.py:92
  36.8 163.7 %while.12 = (s32[]{:T(128)}, bf16[16,512,4096]{2,1,0:T(8,128)(2,1)}, f32[16,16,512]{2,1,0:T(8,128)S(1)}, f32[4096]{0:T(1024)S(1)}, f32[16,4096]{1,0:T(8,128)S(1)}, /*index=5*/s32[]{:T(128)}) while((s32[]{:T(128)}, bf16[16,512,4096]{2,1,0:T(8,128)(2,1)}, f32[16,16,512]{2,1,0:T(8,128)S(1)}, f32[4096]{0:T(1024)S(1)}, f32[16,4096]{1,0:T(8,128)S(1)}, ...), condition=%wide.region_3.4_spmd, body=%wide.region_1.3_spmd.sunk | while | flops 415251968 | bytes 4543561 | solution.py:33
  36.8 10.2 %fusion.25 = bf16[16,512,4096]{2,1,0:T(8,128)(2,1)} fusion(bf16[16,512,4096]{2,1,0:T(8,128)(2,1)} %get-tuple-element.127, s32[]{:T(128)} %get-tuple-element.126, f32[16,4096]{1,0:T(8,128)S(1)} %get-tuple-element.136, f32[4096]{0:T(1024)S(1)} %get-tuple-element.135, f32[512]{0:T(512)S(1)} %fusion.24, f32[16,16,512]{2,1,0:T(8,128)S(1)} %get-tuple-element.134), kind=kOutput, calls=%fused_computation.2.clone.1 | convolution fusion | flops 415236096 | bytes 4508672 | tf_op jit(solution)/shard_map/while/body/eval_jaxpr/dot_general | solution.py:14
  47.1 10.2 %fusion.25 = bf16[16,512,4096]{2,1,0:T(8,128)(2,1)} fusion(bf16[16,512,4096]{2,1,0:T(8,128)(2,1)} %get-tuple-element.127, s32[]{:T(128)} %get-tuple-element.126, f32[16,4096]{1,0:T(8,128)S(1)} %get-tuple-element.136, f32[4096]{0:T(1024)S(1)} %get-tuple-element.135, f32[512]{0:T(512)S(1)} %fusion.24, f32[16,16,512]{2,1,0:T(8,128)S(1)} %get-tuple-element.134), kind=kOutput, calls=%fused_computation.2.clone.1 | convolution fusion | flops 415236096 | bytes 4508672 | tf_op jit(solution)/shard_map/while/body/eval_jaxpr/dot_general | solution.py:14
  57.3 10.2 %fusion.25 = bf16[16,512,4096]{2,1,0:T(8,128)(2,1)} fusion(bf16[16,512,4096]{2,1,0:T(8,128)(2,1)} %get-tuple-element.127, s32[]{:T(128)} %get-tuple-element.126, f32[16,4096]{1,0:T(8,128)S(1)} %get-tuple-element.136, f32[4096]{0:T(1024)S(1)} %get-tuple-element.135, f32[512]{0:T(512)S(1)} %fusion.24, f32[16,16,512]{2,1,0:T(8,128)S(1)} %get-tuple-element.134), kind=kOutput, calls=%fused_computation.2.clone.1 | convolution fusion | flops 415236096 | bytes 4508672 | tf_op jit(solution)/shard_map/while/body/eval_jaxpr/dot_general | solution.py:14
  67.5 10.2 %fusion.25 = bf16[16,512,4096]{2,1,0:T(8,128)(2,1)} fusion(bf16[16,512,4096]{2,1,0:T(8,128)(2,1)} %get-tuple-element.127, s32[]{:T(128)} %get-tuple-element.126, f32[16,4096]{1,0:T(8,128)S(1)} %get-tuple-element.136, f32[4096]{0:T(1024)S(1)} %get-tuple-element.135, f32[512]{0:T(512)S(1)} %fusion.24, f32[16,16,512]{2,1,0:T(8,128)S(1)} %get-tuple-element.134), kind=kOutput, calls=%fused_computation.2.clone.1 | convolution fusion | flops 415236096 | bytes 4508672 | tf_op jit(solution)/shard_map/while/body/eval_jaxpr/dot_general | solution.py:14
  77.8 10.2 %fusion.25 = bf16[16,512,4096]{2,1,0:T(8,128)(2,1)} fusion(bf16[16,512,4096]{2,1,0:T(8,128)(2,1)} %get-tuple-element.127, s32[]{:T(128)} %get-tuple-element.126, f32[16,4096]{1,0:T(8,128)S(1)} %get-tuple-element.136, f32[4096]{0:T(1024)S(1)} %get-tuple-element.135, f32[512]{0:T(512)S(1)} %fusion.24, f32[16,16,512]{2,1,0:T(8,128)S(1)} %get-tuple-element.134), kind=kOutput, calls=%fused_computation.2.clone.1 | convolution fusion | flops 415236096 | bytes 4508672 | tf_op jit(solution)/shard_map/while/body/eval_jaxpr/dot_general | solution.py:14
  88.0 10.2 %fusion.25 = bf16[16,512,4096]{2,1,0:T(8,128)(2,1)} fusion(bf16[16,512,4096]{2,1,0:T(8,128)(2,1)} %get-tuple-element.127, s32[]{:T(128)} %get-tuple-element.126, f32[16,4096]{1,0:T(8,128)S(1)} %get-tuple-element.136, f32[4096]{0:T(1024)S(1)} %get-tuple-element.135, f32[512]{0:T(512)S(1)} %fusion.24, f32[16,16,512]{2,1,0:T(8,128)S(1)} %get-tuple-element.134), kind=kOutput, calls=%fused_computation.2.clone.1 | convolution fusion | flops 415236096 | bytes 4508672 | tf_op jit(solution)/shard_map/while/body/eval_jaxpr/dot_general | solution.py:14
  98.2 10.2 %fusion.25 = bf16[16,512,4096]{2,1,0:T(8,128)(2,1)} fusion(bf16[16,512,4096]{2,1,0:T(8,128)(2,1)} %get-tuple-element.127, s32[]{:T(128)} %get-tuple-element.126, f32[16,4096]{1,0:T(8,128)S(1)} %get-tuple-element.136, f32[4096]{0:T(1024)S(1)} %get-tuple-element.135, f32[512]{0:T(512)S(1)} %fusion.24, f32[16,16,512]{2,1,0:T(8,128)S(1)} %get-tuple-element.134), kind=kOutput, calls=%fused_computation.2.clone.1 | convolution fusion | flops 415236096 | bytes 4508672 | tf_op jit(solution)/shard_map/while/body/eval_jaxpr/dot_general | solution.py:14
  108.4 10.2 %fusion.25 = bf16[16,512,4096]{2,1,0:T(8,128)(2,1)} fusion(bf16[16,512,4096]{2,1,0:T(8,128)(2,1)} %get-tuple-element.127, s32[]{:T(128)} %get-tuple-element.126, f32[16,4096]{1,0:T(8,128)S(1)} %get-tuple-element.136, f32[4096]{0:T(1024)S(1)} %get-tuple-element.135, f32[512]{0:T(512)S(1)} %fusion.24, f32[16,16,512]{2,1,0:T(8,128)S(1)} %get-tuple-element.134), kind=kOutput, calls=%fused_computation.2.clone.1 | convolution fusion | flops 415236096 | bytes 4508672 | tf_op jit(solution)/shard_map/while/body/eval_jaxpr/dot_general | solution.py:14
  118.6 10.3 %fusion.25 = bf16[16,512,4096]{2,1,0:T(8,128)(2,1)} fusion(bf16[16,512,4096]{2,1,0:T(8,128)(2,1)} %get-tuple-element.127, s32[]{:T(128)} %get-tuple-element.126, f32[16,4096]{1,0:T(8,128)S(1)} %get-tuple-element.136, f32[4096]{0:T(1024)S(1)} %get-tuple-element.135, f32[512]{0:T(512)S(1)} %fusion.24, f32[16,16,512]{2,1,0:T(8,128)S(1)} %get-tuple-element.134), kind=kOutput, calls=%fused_computation.2.clone.1 | convolution fusion | flops 415236096 | bytes 4508672 | tf_op jit(solution)/shard_map/while/body/eval_jaxpr/dot_general | solution.py:14
  128.9 10.2 %fusion.25 = bf16[16,512,4096]{2,1,0:T(8,128)(2,1)} fusion(bf16[16,512,4096]{2,1,0:T(8,128)(2,1)} %get-tuple-element.127, s32[]{:T(128)} %get-tuple-element.126, f32[16,4096]{1,0:T(8,128)S(1)} %get-tuple-element.136, f32[4096]{0:T(1024)S(1)} %get-tuple-element.135, f32[512]{0:T(512)S(1)} %fusion.24, f32[16,16,512]{2,1,0:T(8,128)S(1)} %get-tuple-element.134), kind=kOutput, calls=%fused_computation.2.clone.1 | convolution fusion | flops 415236096 | bytes 4508672 | tf_op jit(solution)/shard_map/while/body/eval_jaxpr/dot_general | solution.py:14
  139.2 10.2 %fusion.25 = bf16[16,512,4096]{2,1,0:T(8,128)(2,1)} fusion(bf16[16,512,4096]{2,1,0:T(8,128)(2,1)} %get-tuple-element.127, s32[]{:T(128)} %get-tuple-element.126, f32[16,4096]{1,0:T(8,128)S(1)} %get-tuple-element.136, f32[4096]{0:T(1024)S(1)} %get-tuple-element.135, f32[512]{0:T(512)S(1)} %fusion.24, f32[16,16,512]{2,1,0:T(8,128)S(1)} %get-tuple-element.134), kind=kOutput, calls=%fused_computation.2.clone.1 | convolution fusion | flops 415236096 | bytes 4508672 | tf_op jit(solution)/shard_map/while/body/eval_jaxpr/dot_general | solution.py:14
  149.4 10.2 %fusion.25 = bf16[16,512,4096]{2,1,0:T(8,128)(2,1)} fusion(bf16[16,512,4096]{2,1,0:T(8,128)(2,1)} %get-tuple-element.127, s32[]{:T(128)} %get-tuple-element.126, f32[16,4096]{1,0:T(8,128)S(1)} %get-tuple-element.136, f32[4096]{0:T(1024)S(1)} %get-tuple-element.135, f32[512]{0:T(512)S(1)} %fusion.24, f32[16,16,512]{2,1,0:T(8,128)S(1)} %get-tuple-element.134), kind=kOutput, calls=%fused_computation.2.clone.1 | convolution fusion | flops 415236096 | bytes 4508672 | tf_op jit(solution)/shard_map/while/body/eval_jaxpr/dot_general | solution.py:14
  159.6 10.3 %fusion.25 = bf16[16,512,4096]{2,1,0:T(8,128)(2,1)} fusion(bf16[16,512,4096]{2,1,0:T(8,128)(2,1)} %get-tuple-element.127, s32[]{:T(128)} %get-tuple-element.126, f32[16,4096]{1,0:T(8,128)S(1)} %get-tuple-element.136, f32[4096]{0:T(1024)S(1)} %get-tuple-element.135, f32[512]{0:T(512)S(1)} %fusion.24, f32[16,16,512]{2,1,0:T(8,128)S(1)} %get-tuple-element.134), kind=kOutput, calls=%fused_computation.2.clone.1 | convolution fusion | flops 415236096 | bytes 4508672 | tf_op jit(solution)/shard_map/while/body/eval_jaxpr/dot_general | solution.py:14
  169.9 10.2 %fusion.25 = bf16[16,512,4096]{2,1,0:T(8,128)(2,1)} fusion(bf16[16,512,4096]{2,1,0:T(8,128)(2,1)} %get-tuple-element.127, s32[]{:T(128)} %get-tuple-element.126, f32[16,4096]{1,0:T(8,128)S(1)} %get-tuple-element.136, f32[4096]{0:T(1024)S(1)} %get-tuple-element.135, f32[512]{0:T(512)S(1)} %fusion.24, f32[16,16,512]{2,1,0:T(8,128)S(1)} %get-tuple-element.134), kind=kOutput, calls=%fused_computation.2.clone.1 | convolution fusion | flops 415236096 | bytes 4508672 | tf_op jit(solution)/shard_map/while/body/eval_jaxpr/dot_general | solution.py:14
  180.1 10.2 %fusion.25 = bf16[16,512,4096]{2,1,0:T(8,128)(2,1)} fusion(bf16[16,512,4096]{2,1,0:T(8,128)(2,1)} %get-tuple-element.127, s32[]{:T(128)} %get-tuple-element.126, f32[16,4096]{1,0:T(8,128)S(1)} %get-tuple-element.136, f32[4096]{0:T(1024)S(1)} %get-tuple-element.135, f32[512]{0:T(512)S(1)} %fusion.24, f32[16,16,512]{2,1,0:T(8,128)S(1)} %get-tuple-element.134), kind=kOutput, calls=%fused_computation.2.clone.1 | convolution fusion | flops 415236096 | bytes 4508672 | tf_op jit(solution)/shard_map/while/body/eval_jaxpr/dot_general | solution.py:14
  190.3 10.2 %fusion.25 = bf16[16,512,4096]{2,1,0:T(8,128)(2,1)} fusion(bf16[16,512,4096]{2,1,0:T(8,128)(2,1)} %get-tuple-element.127, s32[]{:T(128)} %get-tuple-element.126, f32[16,4096]{1,0:T(8,128)S(1)} %get-tuple-element.136, f32[4096]{0:T(1024)S(1)} %get-tuple-element.135, f32[512]{0:T(512)S(1)} %fusion.24, f32[16,16,512]{2,1,0:T(8,128)S(1)} %get-tuple-element.134), kind=kOutput, calls=%fused_computation.2.clone.1 | convolution fusion | flops 415236096 | bytes 4508672 | tf_op jit(solution)/shard_map/while/body/eval_jaxpr/dot_general | solution.py:14
  200.5 29.2 %convolution_convert_fusion.2 = bf16[4096,128]{1,0:T(8,128)(2,1)} fusion(bf16[8192,4096]{1,0:T(8,128)(2,1)} %bitcast.3, bf16[8192,128]{1,0:T(8,128)(2,1)} %all-gather.4.cloned.1.call-done), kind=kOutput, calls=%fused_computation.10 | convolution fusion | flops 8590458880 | bytes 70254592 | tf_op jit(solution)/shard_map/dot_general | solution.py:105
  229.7 0.0 reduce-scatter.4.cloned.1.call-update
  229.7 0.0 all-gather.6.cloned.1.call-start
  229.7 28.3 %reduce-scatter.4.cloned.1.call-done = bf16[1024,128]{1,0:T(8,128)(2,1)} async-done(((bf16[4096,128]{1,0:T(8,128)(2,1)}), bf16[1024,128]{1,0:T(8,128)(2,1)}) %reduce-scatter.4.cloned.1.call-update) | async-done | bytes 262160 | tf_op jit(solution)/shard_map/reduce_scatter | solution.py:104
  258.1 1.1 multiply_reduce_fusion.3
  259.2 38.9 %all-reduce.2 = (f32[128]{0:T(128)S(1)}, f32[128]{0:T(128)S(1)}) all-reduce(f32[128]{0:T(128)S(1)} %get-tuple-element.63, f32[128]{0:T(128)S(1)} %get-tuple-element.62), channel_id=1, replica_groups=mesh['row'=4,'col'=8] {'row','col'}, use_global_device_ids=true, to_apply=%region_6.7 | all-reduce | flops 256 | bytes 2048 | tf_op jit(solution)/shard_map/psum | solution.py:114
  298.1 1.9 fusion.10
  299.9 0.0 all-gather.6.cloned.1.call-update
  300.0 0.0 reduce-scatter.6.cloned.1.call-start
  300.0 27.6 %all-gather.6.cloned.1.call-done = bf16[8192,128]{1,0:T(8,128)(2,1)} async-done(((bf16[1024,128]{1,0:T(8,128)(2,1)}), bf16[8192,128]{1,0:T(8,128)(2,1)}) %all-gather.6.cloned.1.call-update) | async-done | bytes 2097168 | tf_op jit(solution)/shard_map/all_gather | solution.py:102
  327.6 29.1 %convolution_convert_fusion.1 = bf16[4096,128]{1,0:T(8,128)(2,1)} fusion(bf16[8192,4096]{1,0:T(8,128)(2,1)} %bitcast.3, bf16[8192,128]{1,0:T(8,128)(2,1)} %all-gather.6.cloned.1.call-done), kind=kOutput, calls=%fused_computation.9 | convolution fusion | flops 8590458880 | bytes 70254592 | tf_op jit(solution)/shard_map/dot_general | solution.py:105
  356.8 0.0 all-gather.8.cloned.1.call-start
  356.8 27.4 %reduce-scatter.6.cloned.1.call-done = bf16[1024,128]{1,0:T(8,128)(2,1)} async-done(((bf16[4096,128]{1,0:T(8,128)(2,1)}), bf16[1024,128]{1,0:T(8,128)(2,1)}) %reduce-scatter.6.cloned.1.call-update) | async-done | bytes 262160 | tf_op jit(solution)/shard_map/reduce_scatter | solution.py:104
  384.2 1.1 multiply_reduce_fusion.2
  385.3 38.7 %all-reduce.1 = (f32[128]{0:T(128)S(1)}, f32[128]{0:T(128)S(1)}) all-reduce(f32[128]{0:T(128)S(1)} %get-tuple-element.61, f32[128]{0:T(128)S(1)} %get-tuple-element.60), channel_id=1, replica_groups=mesh['row'=4,'col'=8] {'row','col'}, use_global_device_ids=true, to_apply=%region_13.14 | all-reduce | flops 256 | bytes 2048 | tf_op jit(solution)/shard_map/psum | solution.py:114
  424.1 1.9 fusion.9
  426.0 0.3 reduce-scatter.8.cloned.1.call-start
  426.3 27.4 %all-gather.8.cloned.1.call-done = bf16[8192,128]{1,0:T(8,128)(2,1)} async-done(((bf16[1024,128]{1,0:T(8,128)(2,1)}), bf16[8192,128]{1,0:T(8,128)(2,1)}) %all-gather.8.cloned.1.call-update) | async-done | bytes 2097168 | tf_op jit(solution)/shard_map/all_gather | solution.py:102
  453.7 29.1 %convolution_convert_fusion = bf16[4096,128]{1,0:T(8,128)(2,1)} fusion(bf16[8192,4096]{1,0:T(8,128)(2,1)} %bitcast.3, bf16[8192,128]{1,0:T(8,128)(2,1)} %all-gather.8.cloned.1.call-done), kind=kOutput, calls=%fused_computation.8 | convolution fusion | flops 8590458880 | bytes 70254592 | tf_op jit(solution)/shard_map/dot_general | solution.py:105
  482.8 0.0 reduce-scatter.8.cloned.1.call-update
  482.8 27.4 %reduce-scatter.8.cloned.1.call-done = bf16[1024,128]{1,0:T(8,128)(2,1)} async-done(((bf16[4096,128]{1,0:T(8,128)(2,1)}), bf16[1024,128]{1,0:T(8,128)(2,1)}) %reduce-scatter.8.cloned.1.call-update) | async-done | bytes 262160 | tf_op jit(solution)/shard_map/reduce_scatter | solution.py:104
  510.3 1.1 multiply_reduce_fusion
  511.4 38.7 %all-reduce = (f32[128]{0:T(128)S(1)}, f32[128]{0:T(128)S(1)}) all-reduce(f32[128]{0:T(128)S(1)} %get-tuple-element.59, f32[128]{0:T(128)S(1)} %get-tuple-element.58), channel_id=1, replica_groups=mesh['row'=4,'col'=8] {'row','col'}, use_global_device_ids=true, to_apply=%region_18.19 | all-reduce | flops 256 | bytes 2048 | tf_op jit(solution)/shard_map/psum | solution.py:114
  550.1 2.0 multiply_add_fusion.1
  (28 shorter events, 0.5 us)
Async XLA Ops:
  7.2 193.3 %all-gather.4.cloned.1.call-start = ((), (), s32[]{:S(2)}) async-start(), calls=%async_computation.3 | async-start | bytes 2359296 | tf_op jit(solution)/shard_map/all_gather | solution.py:102
  9.1 249.0 %reduce-scatter.4.cloned.1.call-start = ((), (), s32[]{:S(2)}) async-start(), calls=%async_computation.4 | async-start | bytes 1310720 | tf_op jit(solution)/shard_map/reduce_scatter | solution.py:104
  200.5 57.5 %copy-start = (s32[1024,128]{1,0:T(8,128)S(1)}, s32[1024,128]{1,0:T(8,128)}, u32[]{:S(2)}) copy-start(s32[1024,128]{1,0:T(8,128)} %param.7) | copy-start | bytes 1572868
  229.7 98.0 %all-gather.6.cloned.1.call-start = ((), (), s32[]{:S(2)}) async-start(), calls=%async_computation.5 | async-start | bytes 2359296 | tf_op jit(solution)/shard_map/all_gather | solution.py:102
  298.1 252.0 %copy-start.1 = (f32[128]{0:T(128)}, f32[128]{0:T(128)S(1)}, u32[]{:S(2)}) copy-start(f32[128]{0:T(128)S(1)} %get-tuple-element.87) | copy-start | bytes 1540
  300.0 84.3 %reduce-scatter.6.cloned.1.call-start = ((), (), s32[]{:S(2)}) async-start(), calls=%async_computation.6 | async-start | bytes 1310720 | tf_op jit(solution)/shard_map/reduce_scatter | solution.py:104
  356.8 96.9 %all-gather.8.cloned.1.call-start = ((), (), s32[]{:S(2)}) async-start(), calls=%async_computation.7 | async-start | bytes 2359296 | tf_op jit(solution)/shard_map/all_gather | solution.py:102
  426.0 84.3 %reduce-scatter.8.cloned.1.call-start = ((), (), s32[]{:S(2)}) async-start(), calls=%async_computation.8 | async-start | bytes 1310720 | tf_op jit(solution)/shard_map/reduce_scatter | solution.py:104
Sparse Core Ops, SparseCore 0:
  9.9 31.1 all-gather.3
  229.8 28.1 reduce-scatter.3
  300.1 27.5 all-gather.5
  356.9 27.2 reduce-scatter.5
  426.1 27.5 all-gather.7
  482.9 27.2 reduce-scatter.7
where the time goes:
time: 560 us; the launch traced here: 559 us
  matrix products  251 us (45%)
  blocking collectives  143 us (26%)
  waiting for transfers between devices  138 us (25%)
  between operations  14.1 us (3%)
  other arithmetic  12.3 us (2%)
    dot_general x16, matrix products, kernel_block(): lax.dot_general(left_points, right_points, (((0,), (0,)), ((), ())), prec...  163 us
    psum x3, blocking collectives, per_device(): curvature = lax.psum(jnp.sum(direction * image, axis=0), ('row', 'col'))  116 us
    dot_general x3, matrix products, per_device(): lax.dot_general(cached, gathered, (((0,), (0,)), ((), ())), preferred_ele...  87.4 us
    reduce_scatter x3, waiting for transfers between devices, per_device(): lax.psum_scatter(lax.dot_general(cached, gathered, (((0,), (0,)), ((), ()...  83.2 us
    all_gather x3, waiting for transfers between devices, per_device(): gathered = lax.all_gather(vector_half, 'col', axis=0, tiled=True)  55.1 us
    all_gather x1, blocking collectives, per_device(): col_points = lax.all_gather(scaled, 'row', axis=1, tiled=True)  15.6 us
  transfers between devices with their start and end apart: 6, of which 5 were waited for; matrix products, arithmetic and copies ran while one was open for 29% of the time, Pallas kernels for 0%

commit v1 on v0

--- a/solution.py
+++ b/solution.py
@@ -111,7 +111,8 @@
             ).astype(jnp.float32)
             + noise_level * direction
         )
-        curvature = lax.psum(jnp.sum(direction * image, axis=0), ("row", "col"))
+        v0 = jnp.sum(direction * image, axis=0)
+        curvature = jax.lax.all_gather(v0, axis_name=("row", "col")).sum(axis=0)
         beta_now = jnp.sqrt(squares + epsilon)
         alpha_now = curvature / (beta_now * beta_now)
         alpha_list.append(alpha_now)

time: 560 us -> 673 us (1.20)
  blocking collectives: 143 us -> 254 us
    all_gather x0 -> x3, blocking collectives: none -> 117 us  [per_device(): curvature = jax.lax.all_gather(v0, axis_name=('row', 'col')).sum(axis=0)]
  transfers between devices with their start and end apart: 6 -> 6, of which waited for: 5 -> 5; matrix products, arithmetic and copies ran while one was open for 29% -> 25% of each run, Pallas kernels for 0% -> 0%
where the time goes in v1:
time: 673 us; the launch traced here: 672 us
  blocking collectives  254 us (38%)
  matrix products  251 us (37%)
  waiting for transfers between devices  140 us (21%)
  between operations  14.1 us (2%)
  other arithmetic  12.5 us (2%)
    dot_general x16, matrix products, kernel_block(): lax.dot_general(left_points, right_points, (((0,), (0,)), ((), ())), prec...  163 us
    all_gather x3, blocking collectives, per_device(): curvature = jax.lax.all_gather(v0, axis_name=('row', 'col')).sum(axis=0)  117 us
    psum x3, blocking collectives, per_device(): squares = lax.psum(jnp.sum(direction * direction, axis=0), ('row', 'col'))  110 us
    dot_general x3, matrix products, per_device(): lax.dot_general(cached, gathered, (((0,), (0,)), ((), ())), preferred_ele...  87.4 us
    reduce_scatter x3, waiting for transfers between devices, per_device(): lax.psum_scatter(lax.dot_general(cached, gathered, (((0,), (0,)), ((), ()...  83.2 us
    all_gather x3, waiting for transfers between devices, per_device(): gathered = lax.all_gather(vector_half, 'col', axis=0, tiled=True)  56.4 us
    all_gather x1, blocking collectives, per_device(): col_points = lax.all_gather(scaled, 'row', axis=1, tiled=True)  15.6 us
  transfers between devices with their start and end apart: 6, of which 5 were waited for; matrix products, arithmetic and copies ran while one was open for 25% of the time, Pallas kernels for 0%

profile of v1, /device:TPU:0, one launch (start us, length us, event | category | flops | bytes accessed | tf_op | source)
XLA Modules:
  0.0 671.9 jit_solution(11850528129935099341)
XLA Ops:
  7.2 1.8 fusion.8
  9.1 0.9 broadcast_multiply_fusion
  10.0 15.6 %all_gather.34 = f32[16,4096]{1,0:T(8,128)S(1)} all-gather(f32[16,1024]{1,0:T(8,128)S(1)} %broadcast_multiply_fusion), channel_id=1, replica_groups=mesh['row'=4,'col'=8] {'row'}, dimensions={1}, use_global_device_ids=true | all-gather | bytes 327680 | tf_op jit(solution)/shard_map/all_gather | solution.py:93
  25.7 11.0 %all_gather.33 = f32[16,8192]{1,0:T(8,128)S(1)} all-gather(f32[16,1024]{1,0:T(8,128)S(1)} %broadcast_multiply_fusion), channel_id=1, replica_groups=mesh['row'=4,'col'=8] {'col'}, dimensions={1}, use_global_device_ids=true | all-gather | bytes 589824 | tf_op jit(solution)/shard_map/all_gather | solution.py:92
  36.8 163.7 %while.12 = (s32[]{:T(128)}, bf16[16,512,4096]{2,1,0:T(8,128)(2,1)}, f32[16,16,512]{2,1,0:T(8,128)S(1)}, f32[4096]{0:T(1024)S(1)}, f32[16,4096]{1,0:T(8,128)S(1)}, /*index=5*/s32[]{:T(128)}) while((s32[]{:T(128)}, bf16[16,512,4096]{2,1,0:T(8,128)(2,1)}, f32[16,16,512]{2,1,0:T(8,128)S(1)}, f32[4096]{0:T(1024)S(1)}, f32[16,4096]{1,0:T(8,128)S(1)}, ...), condition=%wide.region_3.4_spmd, body=%wide.region_1.3_spmd.sunk | while | flops 415251968 | bytes 4543561 | solution.py:33
  36.8 10.2 %fusion.25 = bf16[16,512,4096]{2,1,0:T(8,128)(2,1)} fusion(bf16[16,512,4096]{2,1,0:T(8,128)(2,1)} %get-tuple-element.121, s32[]{:T(128)} %get-tuple-element.120, f32[16,4096]{1,0:T(8,128)S(1)} %get-tuple-element.130, f32[4096]{0:T(1024)S(1)} %get-tuple-element.129, f32[512]{0:T(512)S(1)} %fusion.24, f32[16,16,512]{2,1,0:T(8,128)S(1)} %get-tuple-element.128), kind=kOutput, calls=%fused_computation.2.clone.1 | convolution fusion | flops 415236096 | bytes 4508672 | tf_op jit(solution)/shard_map/while/body/eval_jaxpr/dot_general | solution.py:14
  47.1 10.2 %fusion.25 = bf16[16,512,4096]{2,1,0:T(8,128)(2,1)} fusion(bf16[16,512,4096]{2,1,0:T(8,128)(2,1)} %get-tuple-element.121, s32[]{:T(128)} %get-tuple-element.120, f32[16,4096]{1,0:T(8,128)S(1)} %get-tuple-element.130, f32[4096]{0:T(1024)S(1)} %get-tuple-element.129, f32[512]{0:T(512)S(1)} %fusion.24, f32[16,16,512]{2,1,0:T(8,128)S(1)} %get-tuple-element.128), kind=kOutput, calls=%fused_computation.2.clone.1 | convolution fusion | flops 415236096 | bytes 4508672 | tf_op jit(solution)/shard_map/while/body/eval_jaxpr/dot_general | solution.py:14
  57.3 10.2 %fusion.25 = bf16[16,512,4096]{2,1,0:T(8,128)(2,1)} fusion(bf16[16,512,4096]{2,1,0:T(8,128)(2,1)} %get-tuple-element.121, s32[]{:T(128)} %get-tuple-element.120, f32[16,4096]{1,0:T(8,128)S(1)} %get-tuple-element.130, f32[4096]{0:T(1024)S(1)} %get-tuple-element.129, f32[512]{0:T(512)S(1)} %fusion.24, f32[16,16,512]{2,1,0:T(8,128)S(1)} %get-tuple-element.128), kind=kOutput, calls=%fused_computation.2.clone.1 | convolution fusion | flops 415236096 | bytes 4508672 | tf_op jit(solution)/shard_map/while/body/eval_jaxpr/dot_general | solution.py:14
  67.5 10.2 %fusion.25 = bf16[16,512,4096]{2,1,0:T(8,128)(2,1)} fusion(bf16[16,512,4096]{2,1,0:T(8,128)(2,1)} %get-tuple-element.121, s32[]{:T(128)} %get-tuple-element.120, f32[16,4096]{1,0:T(8,128)S(1)} %get-tuple-element.130, f32[4096]{0:T(1024)S(1)} %get-tuple-element.129, f32[512]{0:T(512)S(1)} %fusion.24, f32[16,16,512]{2,1,0:T(8,128)S(1)} %get-tuple-element.128), kind=kOutput, calls=%fused_computation.2.clone.1 | convolution fusion | flops 415236096 | bytes 4508672 | tf_op jit(solution)/shard_map/while/body/eval_jaxpr/dot_general | solution.py:14
  77.8 10.2 %fusion.25 = bf16[16,512,4096]{2,1,0:T(8,128)(2,1)} fusion(bf16[16,512,4096]{2,1,0:T(8,128)(2,1)} %get-tuple-element.121, s32[]{:T(128)} %get-tuple-element.120, f32[16,4096]{1,0:T(8,128)S(1)} %get-tuple-element.130, f32[4096]{0:T(1024)S(1)} %get-tuple-element.129, f32[512]{0:T(512)S(1)} %fusion.24, f32[16,16,512]{2,1,0:T(8,128)S(1)} %get-tuple-element.128), kind=kOutput, calls=%fused_computation.2.clone.1 | convolution fusion | flops 415236096 | bytes 4508672 | tf_op jit(solution)/shard_map/while/body/eval_jaxpr/dot_general | solution.py:14
  88.0 10.2 %fusion.25 = bf16[16,512,4096]{2,1,0:T(8,128)(2,1)} fusion(bf16[16,512,4096]{2,1,0:T(8,128)(2,1)} %get-tuple-element.121, s32[]{:T(128)} %get-tuple-element.120, f32[16,4096]{1,0:T(8,128)S(1)} %get-tuple-element.130, f32[4096]{0:T(1024)S(1)} %get-tuple-element.129, f32[512]{0:T(512)S(1)} %fusion.24, f32[16,16,512]{2,1,0:T(8,128)S(1)} %get-tuple-element.128), kind=kOutput, calls=%fused_computation.2.clone.1 | convolution fusion | flops 415236096 | bytes 4508672 | tf_op jit(solution)/shard_map/while/body/eval_jaxpr/dot_general | solution.py:14
  98.2 10.2 %fusion.25 = bf16[16,512,4096]{2,1,0:T(8,128)(2,1)} fusion(bf16[16,512,4096]{2,1,0:T(8,128)(2,1)} %get-tuple-element.121, s32[]{:T(128)} %get-tuple-element.120, f32[16,4096]{1,0:T(8,128)S(1)} %get-tuple-element.130, f32[4096]{0:T(1024)S(1)} %get-tuple-element.129, f32[512]{0:T(512)S(1)} %fusion.24, f32[16,16,512]{2,1,0:T(8,128)S(1)} %get-tuple-element.128), kind=kOutput, calls=%fused_computation.2.clone.1 | convolution fusion | flops 415236096 | bytes 4508672 | tf_op jit(solution)/shard_map/while/body/eval_jaxpr/dot_general | solution.py:14
  108.4 10.2 %fusion.25 = bf16[16,512,4096]{2,1,0:T(8,128)(2,1)} fusion(bf16[16,512,4096]{2,1,0:T(8,128)(2,1)} %get-tuple-element.121, s32[]{:T(128)} %get-tuple-element.120, f32[16,4096]{1,0:T(8,128)S(1)} %get-tuple-element.130, f32[4096]{0:T(1024)S(1)} %get-tuple-element.129, f32[512]{0:T(512)S(1)} %fusion.24, f32[16,16,512]{2,1,0:T(8,128)S(1)} %get-tuple-element.128), kind=kOutput, calls=%fused_computation.2.clone.1 | convolution fusion | flops 415236096 | bytes 4508672 | tf_op jit(solution)/shard_map/while/body/eval_jaxpr/dot_general | solution.py:14
  118.6 10.3 %fusion.25 = bf16[16,512,4096]{2,1,0:T(8,128)(2,1)} fusion(bf16[16,512,4096]{2,1,0:T(8,128)(2,1)} %get-tuple-element.121, s32[]{:T(128)} %get-tuple-element.120, f32[16,4096]{1,0:T(8,128)S(1)} %get-tuple-element.130, f32[4096]{0:T(1024)S(1)} %get-tuple-element.129, f32[512]{0:T(512)S(1)} %fusion.24, f32[16,16,512]{2,1,0:T(8,128)S(1)} %get-tuple-element.128), kind=kOutput, calls=%fused_computation.2.clone.1 | convolution fusion | flops 415236096 | bytes 4508672 | tf_op jit(solution)/shard_map/while/body/eval_jaxpr/dot_general | solution.py:14
  128.9 10.2 %fusion.25 = bf16[16,512,4096]{2,1,0:T(8,128)(2,1)} fusion(bf16[16,512,4096]{2,1,0:T(8,128)(2,1)} %get-tuple-element.121, s32[]{:T(128)} %get-tuple-element.120, f32[16,4096]{1,0:T(8,128)S(1)} %get-tuple-element.130, f32[4096]{0:T(1024)S(1)} %get-tuple-element.129, f32[512]{0:T(512)S(1)} %fusion.24, f32[16,16,512]{2,1,0:T(8,128)S(1)} %get-tuple-element.128), kind=kOutput, calls=%fused_computation.2.clone.1 | convolution fusion | flops 415236096 | bytes 4508672 | tf_op jit(solution)/shard_map/while/body/eval_jaxpr/dot_general | solution.py:14
  139.2 10.2 %fusion.25 = bf16[16,512,4096]{2,1,0:T(8,128)(2,1)} fusion(bf16[16,512,4096]{2,1,0:T(8,128)(2,1)} %get-tuple-element.121, s32[]{:T(128)} %get-tuple-element.120, f32[16,4096]{1,0:T(8,128)S(1)} %get-tuple-element.130, f32[4096]{0:T(1024)S(1)} %get-tuple-element.129, f32[512]{0:T(512)S(1)} %fusion.24, f32[16,16,512]{2,1,0:T(8,128)S(1)} %get-tuple-element.128), kind=kOutput, calls=%fused_computation.2.clone.1 | convolution fusion | flops 415236096 | bytes 4508672 | tf_op jit(solution)/shard_map/while/body/eval_jaxpr/dot_general | solution.py:14
  149.4 10.2 %fusion.25 = bf16[16,512,4096]{2,1,0:T(8,128)(2,1)} fusion(bf16[16,512,4096]{2,1,0:T(8,128)(2,1)} %get-tuple-element.121, s32[]{:T(128)} %get-tuple-element.120, f32[16,4096]{1,0:T(8,128)S(1)} %get-tuple-element.130, f32[4096]{0:T(1024)S(1)} %get-tuple-element.129, f32[512]{0:T(512)S(1)} %fusion.24, f32[16,16,512]{2,1,0:T(8,128)S(1)} %get-tuple-element.128), kind=kOutput, calls=%fused_computation.2.clone.1 | convolution fusion | flops 415236096 | bytes 4508672 | tf_op jit(solution)/shard_map/while/body/eval_jaxpr/dot_general | solution.py:14
  159.6 10.3 %fusion.25 = bf16[16,512,4096]{2,1,0:T(8,128)(2,1)} fusion(bf16[16,512,4096]{2,1,0:T(8,128)(2,1)} %get-tuple-element.121, s32[]{:T(128)} %get-tuple-element.120, f32[16,4096]{1,0:T(8,128)S(1)} %get-tuple-element.130, f32[4096]{0:T(1024)S(1)} %get-tuple-element.129, f32[512]{0:T(512)S(1)} %fusion.24, f32[16,16,512]{2,1,0:T(8,128)S(1)} %get-tuple-element.128), kind=kOutput, calls=%fused_computation.2.clone.1 | convolution fusion | flops 415236096 | bytes 4508672 | tf_op jit(solution)/shard_map/while/body/eval_jaxpr/dot_general | solution.py:14
  169.9 10.2 %fusion.25 = bf16[16,512,4096]{2,1,0:T(8,128)(2,1)} fusion(bf16[16,512,4096]{2,1,0:T(8,128)(2,1)} %get-tuple-element.121, s32[]{:T(128)} %get-tuple-element.120, f32[16,4096]{1,0:T(8,128)S(1)} %get-tuple-element.130, f32[4096]{0:T(1024)S(1)} %get-tuple-element.129, f32[512]{0:T(512)S(1)} %fusion.24, f32[16,16,512]{2,1,0:T(8,128)S(1)} %get-tuple-element.128), kind=kOutput, calls=%fused_computation.2.clone.1 | convolution fusion | flops 415236096 | bytes 4508672 | tf_op jit(solution)/shard_map/while/body/eval_jaxpr/dot_general | solution.py:14
  180.1 10.2 %fusion.25 = bf16[16,512,4096]{2,1,0:T(8,128)(2,1)} fusion(bf16[16,512,4096]{2,1,0:T(8,128)(2,1)} %get-tuple-element.121, s32[]{:T(128)} %get-tuple-element.120, f32[16,4096]{1,0:T(8,128)S(1)} %get-tuple-element.130, f32[4096]{0:T(1024)S(1)} %get-tuple-element.129, f32[512]{0:T(512)S(1)} %fusion.24, f32[16,16,512]{2,1,0:T(8,128)S(1)} %get-tuple-element.128), kind=kOutput, calls=%fused_computation.2.clone.1 | convolution fusion | flops 415236096 | bytes 4508672 | tf_op jit(solution)/shard_map/while/body/eval_jaxpr/dot_general | solution.py:14
  190.3 10.2 %fusion.25 = bf16[16,512,4096]{2,1,0:T(8,128)(2,1)} fusion(bf16[16,512,4096]{2,1,0:T(8,128)(2,1)} %get-tuple-element.121, s32[]{:T(128)} %get-tuple-element.120, f32[16,4096]{1,0:T(8,128)S(1)} %get-tuple-element.130, f32[4096]{0:T(1024)S(1)} %get-tuple-element.129, f32[512]{0:T(512)S(1)} %fusion.24, f32[16,16,512]{2,1,0:T(8,128)S(1)} %get-tuple-element.128), kind=kOutput, calls=%fused_computation.2.clone.1 | convolution fusion | flops 415236096 | bytes 4508672 | tf_op jit(solution)/shard_map/while/body/eval_jaxpr/dot_general | solution.py:14
  200.5 29.2 %convolution_convert_fusion.2 = bf16[4096,128]{1,0:T(8,128)(2,1)} fusion(bf16[8192,4096]{1,0:T(8,128)(2,1)} %bitcast.3, bf16[8192,128]{1,0:T(8,128)(2,1)} %all-gather.10.cloned.1.call-done), kind=kOutput, calls=%fused_computation.10 | convolution fusion | flops 8590458880 | bytes 70254592 | tf_op jit(solution)/shard_map/dot_general | solution.py:105
  229.7 0.0 all-gather.12.cloned.1.call-start
  229.7 28.3 %reduce-scatter.4.cloned.1.call-done = bf16[1024,128]{1,0:T(8,128)(2,1)} async-done(((bf16[4096,128]{1,0:T(8,128)(2,1)}), bf16[1024,128]{1,0:T(8,128)(2,1)}) %reduce-scatter.4.cloned.1.call-update) | async-done | bytes 262160 | tf_op jit(solution)/shard_map/reduce_scatter | solution.py:104
  258.1 1.1 multiply_reduce_fusion.3
  259.2 39.2 %all-gather.3 = f32[32,1,128]{2,1,0:T(1,128)S(1)} all-gather(f32[1,1,128]{2,1,0:T(1,128)S(1)} %bitcast.39), channel_id=2, replica_groups=mesh['row'=4,'col'=8] {'row','col'}, dimensions={0}, use_global_device_ids=true | all-gather | bytes 16896 | tf_op jit(solution)/shard_map/all_gather | solution.py:115
  298.4 36.8 %psum.21 = f32[128]{0:T(128)S(1)} all-reduce(f32[128]{0:T(128)S(1)} %get-tuple-element.62), channel_id=1, replica_groups=mesh['row'=4,'col'=8] {'row','col'}, use_global_device_ids=true, to_apply=%region_8.9 | all-reduce | flops 128 | bytes 1024 | tf_op jit(solution)/shard_map/psum | solution.py:100
  335.2 0.1 reduce_sum.105
  335.2 1.9 fusion.10
  337.1 0.0 reduce-scatter.6.cloned.1.call-start
  337.2 28.3 %all-gather.12.cloned.1.call-done = bf16[8192,128]{1,0:T(8,128)(2,1)} async-done(((bf16[1024,128]{1,0:T(8,128)(2,1)}), bf16[8192,128]{1,0:T(8,128)(2,1)}) %all-gather.12.cloned.1.call-update) | async-done | bytes 2097168 | tf_op jit(solution)/shard_map/all_gather | solution.py:102
  365.5 29.1 %convolution_convert_fusion.1 = bf16[4096,128]{1,0:T(8,128)(2,1)} fusion(bf16[8192,4096]{1,0:T(8,128)(2,1)} %bitcast.3, bf16[8192,128]{1,0:T(8,128)(2,1)} %all-gather.12.cloned.1.call-done), kind=kOutput, calls=%fused_computation.9 | convolution fusion | flops 8590458880 | bytes 70254592 | tf_op jit(solution)/shard_map/dot_general | solution.py:105
  394.6 0.0 all-gather.14.cloned.1.call-start
  394.7 27.4 %reduce-scatter.6.cloned.1.call-done = bf16[1024,128]{1,0:T(8,128)(2,1)} async-done(((bf16[4096,128]{1,0:T(8,128)(2,1)}), bf16[1024,128]{1,0:T(8,128)(2,1)}) %reduce-scatter.6.cloned.1.call-update) | async-done | bytes 262160 | tf_op jit(solution)/shard_map/reduce_scatter | solution.py:104
  422.1 1.1 multiply_reduce_fusion.2
  423.2 39.0 %all-gather.4 = f32[32,1,128]{2,1,0:T(1,128)S(1)} all-gather(f32[1,1,128]{2,1,0:T(1,128)S(1)} %bitcast.40), channel_id=3, replica_groups=mesh['row'=4,'col'=8] {'row','col'}, dimensions={0}, use_global_device_ids=true | all-gather | bytes 16896 | tf_op jit(solution)/shard_map/all_gather | solution.py:115
  462.2 0.1 reduce_sum.109
  462.3 36.8 %psum.22 = f32[128]{0:T(128)S(1)} all-reduce(f32[128]{0:T(128)S(1)} %get-tuple-element.60), channel_id=1, replica_groups=mesh['row'=4,'col'=8] {'row','col'}, use_global_device_ids=true, to_apply=%region_10.11 | all-reduce | flops 128 | bytes 1024 | tf_op jit(solution)/shard_map/psum | solution.py:100
  499.1 1.9 fusion.9
  501.0 0.3 reduce-scatter.8.cloned.1.call-start
  501.3 28.1 %all-gather.14.cloned.1.call-done = bf16[8192,128]{1,0:T(8,128)(2,1)} async-done(((bf16[1024,128]{1,0:T(8,128)(2,1)}), bf16[8192,128]{1,0:T(8,128)(2,1)}) %all-gather.14.cloned.1.call-update) | async-done | bytes 2097168 | tf_op jit(solution)/shard_map/all_gather | solution.py:102
  529.4 29.1 %convolution_convert_fusion = bf16[4096,128]{1,0:T(8,128)(2,1)} fusion(bf16[8192,4096]{1,0:T(8,128)(2,1)} %bitcast.3, bf16[8192,128]{1,0:T(8,128)(2,1)} %all-gather.14.cloned.1.call-done), kind=kOutput, calls=%fused_computation.8 | convolution fusion | flops 8590458880 | bytes 70254592 | tf_op jit(solution)/shard_map/dot_general | solution.py:105
  558.5 27.4 %reduce-scatter.8.cloned.1.call-done = bf16[1024,128]{1,0:T(8,128)(2,1)} async-done(((bf16[4096,128]{1,0:T(8,128)(2,1)}), bf16[1024,128]{1,0:T(8,128)(2,1)}) %reduce-scatter.8.cloned.1.call-update) | async-done | bytes 262160 | tf_op jit(solution)/shard_map/reduce_scatter | solution.py:104
  586.0 1.1 multiply_reduce_fusion
  587.1 39.0 %all-gather.5 = f32[32,1,128]{2,1,0:T(1,128)S(1)} all-gather(f32[1,1,128]{2,1,0:T(1,128)S(1)} %bitcast.38), channel_id=4, replica_groups=mesh['row'=4,'col'=8] {'row','col'}, dimensions={0}, use_global_device_ids=true | all-gather | bytes 16896 | tf_op jit(solution)/shard_map/all_gather | solution.py:115
  626.1 0.1 reduce_sum.112
  626.2 36.8 %psum.23 = f32[128]{0:T(128)S(1)} all-reduce(f32[128]{0:T(128)S(1)} %get-tuple-element.58), channel_id=1, replica_groups=mesh['row'=4,'col'=8] {'row','col'}, use_global_device_ids=true, to_apply=%region_15.16 | all-reduce | flops 128 | bytes 1024 | tf_op jit(solution)/shard_map/psum | solution.py:100
  663.0 2.0 multiply_add_fusion.1
  (34 shorter events, 0.7 us)
Async XLA Ops:
  7.2 193.3 %all-gather.10.cloned.1.call-start = ((), (), s32[]{:S(2)}) async-start(), calls=%async_computation.3 | async-start | bytes 2359296 | tf_op jit(solution)/shard_map/all_gather | solution.py:102
  9.1 249.0 %reduce-scatter.4.cloned.1.call-start = ((), (), s32[]{:S(2)}) async-start(), calls=%async_computation.4 | async-start | bytes 1310720 | tf_op jit(solution)/shard_map/reduce_scatter | solution.py:104
  200.5 57.5 %copy-start = (s32[1024,128]{1,0:T(8,128)S(1)}, s32[1024,128]{1,0:T(8,128)}, u32[]{:S(2)}) copy-start(s32[1024,128]{1,0:T(8,128)} %param.7) | copy-start | bytes 1572868
  229.7 135.8 %all-gather.12.cloned.1.call-start = ((), (), s32[]{:S(2)}) async-start(), calls=%async_computation.5 | async-start | bytes 2359296 | tf_op jit(solution)/shard_map/all_gather | solution.py:102
  335.2 327.8 %copy-start.1 = (f32[128]{0:T(128)}, f32[128]{0:T(128)S(1)}, u32[]{:S(2)}) copy-start(f32[128]{0:T(128)S(1)} %get-tuple-element.81) | copy-start | bytes 1540
  337.1 84.9 %reduce-scatter.6.cloned.1.call-start = ((), (), s32[]{:S(2)}) async-start(), calls=%async_computation.6 | async-start | bytes 1310720 | tf_op jit(solution)/shard_map/reduce_scatter | solution.py:104
  394.6 134.8 %all-gather.14.cloned.1.call-start = ((), (), s32[]{:S(2)}) async-start(), calls=%async_computation.7 | async-start | bytes 2359296 | tf_op jit(solution)/shard_map/all_gather | solution.py:102
  501.0 84.9 %reduce-scatter.8.cloned.1.call-start = ((), (), s32[]{:S(2)}) async-start(), calls=%async_computation.8 | async-start | bytes 1310720 | tf_op jit(solution)/shard_map/reduce_scatter | solution.py:104
Sparse Core Ops, SparseCore 0:
  9.9 31.1 all-gather.9
  229.8 28.1 reduce-scatter.3
  337.2 28.1 all-gather.11
  394.7 27.2 reduce-scatter.5
  501.2 28.1 all-gather.13
  558.7 27.2 reduce-scatter.7
